TPU v7x, 32 devices: a whole 2x2x4 slice. The times are simulated.
32 devices in a mesh: section: 4 (over y, x), chan: 8 (over z, core).
Axes of the slice: x: 2, y: 2, z: 4, core: 2. Of those that a mesh axis runs over, the one named last changes fastest.
Arguments:
- voltages: bfloat16 [2, 512, 524288], P(None, 'chan', 'section'), may hold values from -6 to 6
- usable: int32 [4096, 512], P(('section', 'chan')), may hold values 0 or 1
- auto_power: float32 [4096, 512], P(('section', 'chan')), may hold values from 0.5 to 4
Outputs:
- gains: float32 [2, 4096, 512], P(None, ('section', 'chan'))
Inputs may be any that keep to these rules, and one draw needn't show every extreme that they name: 1 marks a feed as usable in that channel, 0 as flagged.
All inputs are finite; a program needn't handle non-finite values. No bound on the sum of `usable` on one device may be relied on, other than what follows from the above.
Results may differ from a plain program's by a relative error of at most 0.0046.
Values may be sent and summed in bfloat16 or wider, within the bound.
A program may use at most 576 MiB of HBM per device.

v0:
```python
import math
import jax
import jax.numpy as jnp
from jax import lax
from jax.sharding import PartitionSpec as P

CHANNELS = 4096
TAPS = 4
ITERS = 5
LANES = 128
epsilon = 1e-06


def shifted_2(block, axis, distance):
    devices = range(lax.axis_size(axis))
    route = [(i - distance, i) for i in devices if i - distance in devices]
    return lax.ppermute(block, axis, route)


def prototype(tap_count, channels):
    position = lax.iota(jnp.float32, tap_count * channels)
    offset = (position - 0.5 * tap_count * channels + 0.5) / channels
    window = 0.5 - 0.5 * jnp.cos(2.0 * jnp.pi * (position + 0.5) / (tap_count * channels))
    return (jnp.sin(jnp.pi * offset) / (jnp.pi * offset) * window).reshape(tap_count, channels)


def first_table(outer):
    index = lax.iota(jnp.int32, outer)
    angles = (index[:, None] * index[None, :] % outer).astype(jnp.float32) * (2.0 * math.pi / outer)
    cosine, sine = (jnp.cos(angles), jnp.sin(angles))
    return jnp.stack(
        [jnp.stack([cosine, -sine], axis=1), jnp.stack([sine, cosine], axis=1)], axis=0
    )


def second_table(outer, inner, factor):
    k = lax.iota(jnp.int32, outer)[:, None, None]
    n = lax.iota(jnp.int32, inner)[None, :, None]
    j = lax.iota(jnp.int32, inner)[None, None, :]
    length = outer * inner
    angles = (n * (j * outer + k) % length).astype(jnp.float32) * (2.0 * math.pi / length)
    cosine, sine = (jnp.cos(angles) * factor, jnp.sin(angles) * factor)
    return jnp.stack(
        [jnp.stack([cosine, -sine], axis=2), jnp.stack([sine, cosine], axis=2)], axis=1
    )


def channelize(voltages, history):
    feeds_here = voltages.shape[1]
    blocks = voltages.shape[2] // CHANNELS
    outer = CHANNELS // LANES
    extended = jnp.concatenate([history, voltages], axis=2)
    extended = extended.reshape(2, feeds_here, blocks + TAPS - 1, outer, LANES)
    extended = extended.transpose(0, 3, 2, 1, 4).astype(jnp.float32)
    coeffs = prototype(TAPS, CHANNELS).reshape(TAPS, 1, outer, 1, 1, LANES)
    filtered = coeffs[0] * extended[:, :, 0:blocks]
    for tap_index in range(1, TAPS):
        filtered = filtered + coeffs[tap_index] * extended[:, :, tap_index : tap_index + blocks]
    halfway = jnp.einsum(
        "pmbfn,pmqk->kqbfn", filtered, first_table(outer), precision=lax.Precision.HIGH
    )
    table = second_table(outer, LANES, 1.0 / math.sqrt(CHANNELS))
    spectra = jnp.einsum("kqbfn,kqnrj->krbfj", halfway, table, precision=lax.Precision.HIGH)
    return spectra.astype(jnp.bfloat16)


def local(voltages, usable, auto_power):
    outer = CHANNELS // LANES
    margin = (TAPS - 1) * CHANNELS
    tail_samples = voltages[:, :, voltages.shape[2] - margin :]
    history = shifted_2(tail_samples, "section", 1)
    small = jnp.stack([usable.astype(jnp.float32), auto_power], axis=0)
    small = lax.all_to_all(small, "chan", split_axis=2, concat_axis=1, tiled=True)
    small = lax.all_gather(small, "section", axis=1, tiled=True)
    feeds_here = small.shape[2]
    small = small.reshape(2, LANES, outer, feeds_here).transpose(0, 2, 3, 1)
    weight, power = (small[0], small[1])
    spectra = channelize(voltages, history)
    blocks = spectra.shape[2]
    real = spectra[:, 0].astype(jnp.float32)
    imag = spectra[:, 1].astype(jnp.float32)
    shifted = blocks * power - jnp.sum(real * real + imag * imag, axis=1)
    now_r, now_i = (weight, jnp.zeros_like(weight))
    for iteration in range(ITERS):
        ur, ui = (now_r[:, None], now_i[:, None])
        proj_r = jnp.sum(real * ur + imag * ui, axis=2)
        proj_i = jnp.sum(real * ui - imag * ur, axis=2)
        rows = [proj_r, proj_i]
        if iteration > 0:
            rows.append(jnp.sum(now_r * now_r + now_i * now_i, axis=1)[:, None])
        rows = lax.psum(jnp.concatenate(rows, axis=1), "chan")
        if iteration > 0:
            inverse = 1.0 / jnp.sqrt(rows[:, 2 * blocks :] + epsilon)
            rows = rows[:, : 2 * blocks] * inverse
            now_r, now_i = (now_r * inverse, now_i * inverse)
        pr, pi = (rows[:, :blocks, None], rows[:, blocks:, None])
        back_r = jnp.sum(real * pr - imag * pi, axis=1)
        back_i = jnp.sum(real * pi + imag * pr, axis=1)
        back_r = weight * (back_r + shifted * (weight * now_r))
        back_i = weight * (back_i + shifted * (weight * now_i))
        result = jnp.stack([back_r, back_i], axis=0)
        if iteration < ITERS - 1:
            now_r, now_i = lax.psum(result, "section")
    result = result.transpose(0, 3, 1, 2).reshape(2, CHANNELS, feeds_here)
    result = lax.psum_scatter(result, "section", scatter_dimension=1, tiled=True)
    result = lax.all_to_all(result, "chan", split_axis=1, concat_axis=2, tiled=True)
    length = jnp.sqrt(jnp.sum(result * result, axis=(0, 2)) + epsilon)
    return result / jnp.sqrt(length)[None, :, None]


def solution(mesh):
    in_specs = (
        P(None, "chan", "section"),
        P(("section", "chan"), None),
        P(("section", "chan"), None),
    )
    out_specs = P(None, ("section", "chan"), None)
    return jax.shard_map(local, mesh=mesh, in_specs=in_specs, out_specs=out_specs, check_vma=False)
```

profile of v0, /device:TPU:0, one launch (start us, length us, event | category | flops | bytes accessed | tf_op | source)
XLA Modules:
  0.0 1319.0 jit_solution(3367526858844399999)
XLA Ops:
  41.7 58.0 %collective-permute-done = bf16[2,64,12288]{2,1,0:T(8,128)(2,1)} collective-permute-done((bf16[2,64,12288]{2,1,0:T(8,128)(2,1)}, bf16[2,64,12288]{2,1,0:T(8,128)(2,1)}, u32[]{:S(2)}, u32[]{:S(2)}) %collective-permute-start) | collective-permute-done | bytes 3145760 | tf_op jit(solution)/shard_map/ppermute | solution.py:17
  99.7 35.9 %maximum_convert_fusion = f32[2,64,143360]{2,1,0:T(8,128)} fusion(bf16[2,64,131072]{2,1,0:T(8,128)(2,1)} %param.3, bf16[2,64,12288]{2,1,0:T(8,128)(2,1)} %collective-permute-done), kind=kLoop, calls=%fused_computation.55 | loop fusion | flops 73400320 | bytes 110100480 | tf_op jit(solution)/shard_map/convert_element_type | solution.py:54
  135.7 48.6 %copy.67 = f32[16,8,1120,128]{3,2,1,0:T(8,128)} copy(f32[16,8,1120,128]{3,1,2,0:T(8,128)} %bitcast.80) | data formatting | bytes 146800640
  184.3 47.7 %copy.76 = f32[2,64,35,32,128]{4,3,0,1,2:T(8,128)} copy(f32[2,64,35,32,128]{4,3,2,1,0:T(8,128)} %bitcast.82) | data formatting | bytes 146800640 | tf_op jit(solution)/shard_map/convert_element_type | solution.py:54
  232.0 112.2 %fusion.57 = f32[32,2,32,64,128,1]{4,0,3,2,1,5:T(8,128)} fusion(f32[2,32,35,64,128]{4,1,0,3,2:T(8,128)} %bitcast.269, f32[32,128]{1,0:T(8,128)S(1)} %get-tuple-element.57, f32[32,128]{1,0:T(8,128)S(1)} %get-tuple-element.58, f32[32,128]{1,0:T(8,128)S(1)} %get-tuple-element.59, f32[32,128]{1,0:T(8,128)S(1)} %get-tuple-element.56, ...), kind=kOutput, calls=%fused_computation.103 | convolution fusion | flops 6559895552 | bytes 335626240 | tf_op jit(solution)/shard_map/pmbfn,pmqk->kqbfn/dot_general | solution.py:59
  344.3 65.4 %fusion.10 = bf16[32,2,32,64,128]{4,3,2,1,0:T(8,128)(2,1)} fusion(f32[32,2,32,64,128,1]{4,0,3,2,1,5:T(8,128)} %fusion.57, f32[32,1,128,2,128]{4,2,1,3,0:T(8,128)} %get-tuple-element.45, f32[32,1,128,2,128]{4,2,1,3,0:T(8,128)} %get-tuple-element.44), kind=kOutput, calls=%fused_computation.56 | convolution fusion | flops 25788678144 | bytes 109051904 | tf_op jit(solution)/shard_map/kqbfn,kqnrj->krbfj/dot_general | solution.py:63
  417.4 21.4 %fusion.12 = (f32[32,32,128]{2,1,0:T(8,128)S(1)}, f32[32,32,128]{2,1,0:T(8,128)S(1)}) fusion(f32[32,64,128]{2,1,0:T(8,128)S(1)} %slice_bitcast_fusion.10, bf16[32,2,32,64,128]{4,3,2,1,0:T(8,128)(2,1)} %fusion.10), kind=kLoop, calls=%fused_computation.58 | loop fusion | flops 83623936 | bytes 35651584 | tf_op jit(solution)/shard_map/reduce_sum | solution.py:86
  440.5 61.3 %all-reduce.10.cloned.1.call-done = f32[32,64,128]{2,1,0:T(8,128)} async-done(((f32[32,64,128]{2,1,0:T(8,128)}), f32[32,64,128]{2,1,0:T(8,128)}) %all-reduce.10.cloned.1.call-update) | async-done | bytes 1048592 | tf_op jit(solution)/shard_map/psum | solution.py:91
  503.0 18.9 %fusion.16 = (f32[32,64,128]{2,1,0:T(8,128)S(1)}, f32[32,64,128]{2,1,0:T(8,128)S(1)}, f32[32,64,128]{2,1,0:T(8,128)S(1)}) fusion(f32[32,32,128]{2,1,0:T(8,128)S(1)} %get-tuple-element.55, f32[32,32,128]{2,1,0:T(8,128)S(1)} %get-tuple-element.54, bf16[32,2,32,64,128]{4,3,2,1,0:T(8,128)(2,1)} %fusion.10), kind=kLoop, calls=%fused_computation.62 | loop fusion | flops 116654080 | bytes 37748736 | tf_op jit(solution)/shard_map/reduce_sum | solution.py:97
  524.3 68.7 %all-reduce.12.cloned.1.call-done = f32[2,32,64,128]{3,2,1,0:T(8,128)} async-done(((f32[2,32,64,128]{3,2,1,0:T(8,128)}), f32[2,32,64,128]{3,2,1,0:T(8,128)}) %all-reduce.12.cloned.1.call-update) | async-done | bytes 2097168 | tf_op jit(solution)/shard_map/psum | solution.py:103
  596.7 21.2 %fusion.22 = (f32[32,32,128]{2,1,0:T(8,128)S(1)}, f32[32,32,128]{2,1,0:T(8,128)S(1)}) fusion(f32[32,64,128]{2,1,0:T(8,128)S(1)} %get-tuple-element.43, f32[32,64,128]{2,1,0:T(8,128)S(1)} %get-tuple-element.42, bf16[32,2,32,64,128]{4,3,2,1,0:T(8,128)(2,1)} %fusion.10), kind=kLoop, calls=%fused_computation.68 | loop fusion | flops 83623936 | bytes 36700160 | tf_op jit(solution)/shard_map/reduce_sum | solution.py:86
  619.2 60.0 %all-reduce.14.cloned.1.call-done = f32[32,65,128]{2,1,0:T(8,128)} async-done(((f32[32,65,128]{2,1,0:T(8,128)}), f32[32,65,128]{2,1,0:T(8,128)}) %all-reduce.14.cloned.1.call-update) | async-done | bytes 1064976 | tf_op jit(solution)/shard_map/psum | solution.py:91
  700.7 68.4 %all-reduce.16.cloned.1.call-done = f32[2,32,64,128]{3,2,1,0:T(8,128)} async-done(((f32[2,32,64,128]{3,2,1,0:T(8,128)}), f32[2,32,64,128]{3,2,1,0:T(8,128)}) %all-reduce.16.cloned.1.call-update) | async-done | bytes 2097168 | tf_op jit(solution)/shard_map/psum | solution.py:103
  772.9 21.2 %fusion.30 = (f32[32,32,128]{2,1,0:T(8,128)S(1)}, f32[32,32,128]{2,1,0:T(8,128)S(1)}) fusion(f32[32,64,128]{2,1,0:T(8,128)S(1)} %get-tuple-element.41, f32[32,64,128]{2,1,0:T(8,128)S(1)} %get-tuple-element.40, bf16[32,2,32,64,128]{4,3,2,1,0:T(8,128)(2,1)} %fusion.10), kind=kLoop, calls=%fused_computation.76 | loop fusion | flops 83623936 | bytes 36700160 | tf_op jit(solution)/shard_map/reduce_sum | solution.py:86
  795.3 60.0 %all-reduce.18.cloned.1.call-done = f32[32,65,128]{2,1,0:T(8,128)} async-done(((f32[32,65,128]{2,1,0:T(8,128)}), f32[32,65,128]{2,1,0:T(8,128)}) %all-reduce.18.cloned.1.call-update) | async-done | bytes 1064976 | tf_op jit(solution)/shard_map/psum | solution.py:91
  857.8 16.5 %fusion.34 = (f32[32,64,128]{2,1,0:T(8,128)S(1)}, f32[32,64,128]{2,1,0:T(8,128)S(1)}) fusion(f32[32,32,128]{2,1,0:T(8,128)S(1)} %get-tuple-element.51, f32[32,32,128]{2,1,0:T(8,128)S(1)} %get-tuple-element.50, bf16[32,2,32,64,128]{4,3,2,1,0:T(8,128)(2,1)} %fusion.10), kind=kLoop, calls=%fused_computation.80 | loop fusion | flops 83361792 | bytes 36700160 | tf_op jit(solution)/shard_map/reduce_sum | solution.py:97
  876.7 68.6 %all-reduce.20.cloned.1.call-done = f32[2,32,64,128]{3,2,1,0:T(8,128)} async-done(((f32[2,32,64,128]{3,2,1,0:T(8,128)}), f32[2,32,64,128]{3,2,1,0:T(8,128)}) %all-reduce.20.cloned.1.call-update) | async-done | bytes 2097168 | tf_op jit(solution)/shard_map/psum | solution.py:103
  949.0 21.2 %fusion.38 = (f32[32,32,128]{2,1,0:T(8,128)S(1)}, f32[32,32,128]{2,1,0:T(8,128)S(1)}) fusion(f32[32,64,128]{2,1,0:T(8,128)S(1)} %get-tuple-element.39, f32[32,64,128]{2,1,0:T(8,128)S(1)} %get-tuple-element.38, bf16[32,2,32,64,128]{4,3,2,1,0:T(8,128)(2,1)} %fusion.10), kind=kLoop, calls=%fused_computation.84 | loop fusion | flops 83623936 | bytes 36700160 | tf_op jit(solution)/shard_map/reduce_sum | solution.py:86
  971.5 60.0 %all-reduce.22.cloned.1.call-done = f32[32,65,128]{2,1,0:T(8,128)} async-done(((f32[32,65,128]{2,1,0:T(8,128)}), f32[32,65,128]{2,1,0:T(8,128)}) %all-reduce.22.cloned.1.call-update) | async-done | bytes 1064976 | tf_op jit(solution)/shard_map/psum | solution.py:91
  1053.0 68.4 %all-reduce.24.cloned.1.call-done = f32[2,32,64,128]{3,2,1,0:T(8,128)} async-done(((f32[2,32,64,128]{3,2,1,0:T(8,128)}), f32[2,32,64,128]{3,2,1,0:T(8,128)}) %all-reduce.24.cloned.1.call-update) | async-done | bytes 2097168 | tf_op jit(solution)/shard_map/psum | solution.py:103
  1125.2 21.2 %fusion.46 = (f32[32,32,128]{2,1,0:T(8,128)S(1)}, f32[32,32,128]{2,1,0:T(8,128)S(1)}) fusion(f32[32,64,128]{2,1,0:T(8,128)S(1)} %get-tuple-element.37, f32[32,64,128]{2,1,0:T(8,128)S(1)} %get-tuple-element.36, bf16[32,2,32,64,128]{4,3,2,1,0:T(8,128)(2,1)} %fusion.10), kind=kLoop, calls=%fused_computation.92 | loop fusion | flops 83623936 | bytes 36700160 | tf_op jit(solution)/shard_map/reduce_sum | solution.py:86
  1147.6 60.0 %all-reduce.26.cloned.1.call-done = f32[32,65,128]{2,1,0:T(8,128)} async-done(((f32[32,65,128]{2,1,0:T(8,128)}), f32[32,65,128]{2,1,0:T(8,128)}) %all-reduce.26.cloned.1.call-update) | async-done | bytes 1064976 | tf_op jit(solution)/shard_map/psum | solution.py:91
  1232.0 51.8 %reduce-scatter.2.cloned.1.call-done = f32[2,1024,64]{2,1,0:T(8,128)} async-done(((f32[2,4096,64]{2,1,0:T(8,128)}), f32[2,1024,64]{2,1,0:T(8,128)}) %reduce-scatter.2.cloned.1.call-update) | async-done | bytes 524304 | tf_op jit(solution)/shard_map/reduce_scatter | solution.py:105
  1286.9 20.0 %all_to_all.36 = f32[8,1,16384]{2,1,0:T(1,128)S(1)} all-to-all(f32[8,1,16384]{2,1,0:T(1,128)S(1)} %reshape.301), channel_id=1, replica_groups=mesh['section'=4,'chan'=8] {'chan'}, dimensions={0} | all-to-all | bytes 1048576 | tf_op jit(solution)/shard_map/all_to_all | solution.py:106
  (113 shorter events, 148.4 us)
Async XLA Ops:
  10.3 89.4 %collective-permute-start = (bf16[2,64,12288]{2,1,0:T(8,128)(2,1)}, bf16[2,64,12288]{2,1,0:T(8,128)(2,1)}, u32[]{:S(2)}, u32[]{:S(2)}) collective-permute-start(bf16[2,64,12288]{2,1,0:T(8,128)(2,1)} %slice.103), channel_id=1, source_target_pairs={{0,8},{8,16},{16,24},{1,9},{9,17},{17,25},{2,10},{10,18},{18,26},{... | collective-permute-start | bytes 9437192 | tf_op jit(solution)/shard_map/ppermute | solution.py:17
  20.4 20.2 %all-to-all-start = ((f32[2,128,512]{1,0,2:T(2,128)}), f32[2,128,512]{1,0,2:T(2,128)S(1)}, u32[]{:S(2)}, u32[]{:S(2)}) async-start(f32[2,128,512]{1,0,2:T(2,128)} %pad_maximum_fusion.9), calls=%async_computation | async-start | bytes 1048576 | tf_op jit(solution)/shard_map/all_to_all | solution.py:73
  25.2 384.4 %all-gather.2.cloned.1.call-start = ((), (), s32[]{:S(2)}) async-start(), calls=%async_computation.3 | async-start | bytes 2621440 | tf_op jit(solution)/shard_map/all_gather | solution.py:74
  41.5 460.2 %all-reduce.10.cloned.1.call-start = ((), (), s32[]{:S(2)}) async-start(), calls=%async_computation.4 | async-start | bytes 2097152 | tf_op jit(solution)/shard_map/psum | solution.py:91
  440.0 153.0 %all-reduce.12.cloned.1.call-start = ((), (), s32[]{:S(2)}) async-start(), calls=%async_computation.5 | async-start | bytes 4194304 | tf_op jit(solution)/shard_map/psum | solution.py:103
  524.3 154.9 %all-reduce.14.cloned.1.call-start = ((), (), s32[]{:S(2)}) async-start(), calls=%async_computation.6 | async-start | bytes 2359296 | tf_op jit(solution)/shard_map/psum | solution.py:91
  619.1 150.0 %all-reduce.16.cloned.1.call-start = ((), (), s32[]{:S(2)}) async-start(), calls=%async_computation.7 | async-start | bytes 4194304 | tf_op jit(solution)/shard_map/psum | solution.py:103
  679.1 19.0 %copy-start.1 = (f32[2,32,64,128]{3,2,1,0:T(8,128)S(1)}, f32[2,32,64,128]{3,2,1,0:T(8,128)}, u32[]{:S(2)}) copy-start(f32[2,32,64,128]{3,2,1,0:T(8,128)} %all-reduce.12.cloned.1.call-done) | copy-start | bytes 6291460
  700.5 154.8 %all-reduce.18.cloned.1.call-start = ((), (), s32[]{:S(2)}) async-start(), calls=%async_computation.8 | async-start | bytes 2359296 | tf_op jit(solution)/shard_map/psum | solution.py:91
  795.3 150.0 %all-reduce.20.cloned.1.call-start = ((), (), s32[]{:S(2)}) async-start(), calls=%async_computation.9 | async-start | bytes 4194304 | tf_op jit(solution)/shard_map/psum | solution.py:103
  855.3 19.0 %copy-start.2 = (f32[2,32,64,128]{3,2,1,0:T(8,128)S(1)}, f32[2,32,64,128]{3,2,1,0:T(8,128)}, u32[]{:S(2)}) copy-start(f32[2,32,64,128]{3,2,1,0:T(8,128)} %all-reduce.16.cloned.1.call-done) | copy-start | bytes 6291460
  876.6 154.8 %all-reduce.22.cloned.1.call-start = ((), (), s32[]{:S(2)}) async-start(), calls=%async_computation.10 | async-start | bytes 2359296 | tf_op jit(solution)/shard_map/psum | solution.py:91
  971.4 150.0 %all-reduce.24.cloned.1.call-start = ((), (), s32[]{:S(2)}) async-start(), calls=%async_computation.11 | async-start | bytes 4194304 | tf_op jit(solution)/shard_map/psum | solution.py:103
  1031.4 19.0 %copy-start.3 = (f32[2,32,64,128]{3,2,1,0:T(8,128)S(1)}, f32[2,32,64,128]{3,2,1,0:T(8,128)}, u32[]{:S(2)}) copy-start(f32[2,32,64,128]{3,2,1,0:T(8,128)} %all-reduce.20.cloned.1.call-done) | copy-start | bytes 6291460
  1052.8 154.8 %all-reduce.26.cloned.1.call-start = ((), (), s32[]{:S(2)}) async-start(), calls=%async_computation.12 | async-start | bytes 2359296 | tf_op jit(solution)/shard_map/psum | solution.py:91
  1147.6 136.2 %reduce-scatter.2.cloned.1.call-start = ((), (), s32[]{:S(2)}) async-start(), calls=%async_computation.13 | async-start | bytes 5242880 | tf_op jit(solution)/shard_map/reduce_scatter | solution.py:105
  1207.6 19.0 %copy-start = (f32[2,32,64,128]{3,2,1,0:T(8,128)S(1)}, f32[2,32,64,128]{3,2,1,0:T(8,128)}, u32[]{:S(2)}) copy-start(f32[2,32,64,128]{3,2,1,0:T(8,128)} %all-reduce.24.cloned.1.call-done) | copy-start | bytes 6291460
Sparse Core Ops, SparseCore 0:
  41.6 49.6 all-gather.1
  440.1 61.5 all-reduce.9
  524.4 68.5 all-reduce.11
  619.3 59.8 all-reduce.13
  700.6 68.5 all-reduce.15
  795.4 59.8 all-reduce.17
  876.7 68.5 all-reduce.19
  971.6 59.8 all-reduce.21
  1052.9 68.5 all-reduce.23
  1147.7 59.8 all-reduce.25
  1232.1 51.6 reduce-scatter.1
where the time goes:
time: 1330 us; the launch traced here: 1320 us
  waiting for transfers between devices  687 us (52%)
  other arithmetic  276 us (21%)
  matrix products  178 us (13%)
  local copies, waits for them, and re-layouts  131 us (10%)
  blocking collectives  20 us (2%)
  between operations  14 us (1%)
    psum x5, waiting for transfers between devices, local(): rows = lax.psum(jnp.concatenate(rows, axis=1), 'chan')  301 us
    psum x4, waiting for transfers between devices, local(): now_r, now_i = lax.psum(result, 'section')  274 us
    dot_general x1, matrix products, channelize(): jnp.einsum('pmbfn,pmqk->kqbfn', filtered, first_table(outer), precision=l...  112 us
    reduce_sum x5, other arithmetic, local(): proj_r = jnp.sum(real * ur + imag * ui, axis=2)  106 us
    reduce_sum x5, other arithmetic, local(): back_r = jnp.sum(real * pr - imag * pi, axis=1)  84.8 us
    dot_general x1, matrix products, channelize(): jnp.einsum('kqbfn,kqnrj->krbfj', halfway, table, precision=lax.Precision....  65.4 us
    ppermute x1, waiting for transfers between devices, shifted_2(): return lax.ppermute(block, axis, route)  58 us
    unnamed x17, local copies, waits for them, and re-layouts  53 us
  transfers between devices with their start and end apart: 13, of which 12 were waited for; matrix products, arithmetic and copies ran while one was open for 25% of the time, Pallas kernels for 0%

commit v1 on v0

--- a/solution.py
+++ b/solution.py
@@ -1,14 +1,23 @@
+import functools
 import math
 import jax
 import jax.numpy as jnp
 from jax import lax
 from jax.sharding import PartitionSpec as P
+from jax.lax import all_gather
 
 CHANNELS = 4096
 TAPS = 4
 ITERS = 5
 LANES = 128
 epsilon = 1e-06
+
+
+def spans_guide(load, across):
+    return all_gather(load, across).sum(axis=0)
+
+
+review_axis_part = functools.partial(spans_guide, across="chan")
 
 
 def shifted_2(block, axis, distance):
@@ -88,7 +97,7 @@
         rows = [proj_r, proj_i]
         if iteration > 0:
             rows.append(jnp.sum(now_r * now_r + now_i * now_i, axis=1)[:, None])
-        rows = lax.psum(jnp.concatenate(rows, axis=1), "chan")
+        rows = review_axis_part(jnp.concatenate(rows, axis=1))
         if iteration > 0:
             inverse = 1.0 / jnp.sqrt(rows[:, 2 * blocks :] + epsilon)
             rows = rows[:, : 2 * blocks] * inverse

time: 1330 us -> 1460 us (1.098)
  waiting for transfers between devices: 687 us -> 797 us
  other arithmetic: 276 us -> 295 us
    all_gather x0 -> x5, waiting for transfers between devices: none -> 416 us  [spans_guide(): return all_gather(load, across).sum(axis=0)]
    psum x5 -> x0, waiting for transfers between devices: 301 us -> none  [local(): rows = lax.psum(jnp.concatenate(rows, axis=1), 'chan')]
    reduce_sum x0 -> x5, other arithmetic: none -> 26.9 us  [spans_guide(): return all_gather(load, across).sum(axis=0)]
    unnamed x17 -> x21, local copies, waits for them, and re-layouts: 53 us -> 52.7 us
  transfers between devices with their start and end apart: 13 -> 13, of which waited for: 12 -> 12; matrix products, arithmetic and copies ran while one was open for 25% -> 23% of each run, Pallas kernels for 0% -> 0%
where the time goes in v1:
time: 1460 us; the launch traced here: 1450 us
  waiting for transfers between devices  797 us (55%)
  other arithmetic  295 us (20%)
  matrix products  178 us (12%)
  local copies, waits for them, and re-layouts  136 us (9%)
  blocking collectives  19.7 us (1%)
    all_gather x5, waiting for transfers between devices, spans_guide(): return all_gather(load, across).sum(axis=0)  416 us
    psum x4, waiting for transfers between devices, local(): now_r, now_i = lax.psum(result, 'section')  272 us
    dot_general x1, matrix products, channelize(): jnp.einsum('pmbfn,pmqk->kqbfn', filtered, first_table(outer), precision=l...  112 us
    reduce_sum x5, other arithmetic, local(): proj_r = jnp.sum(real * ur + imag * ui, axis=2)  107 us
    reduce_sum x5, other arithmetic, local(): back_r = jnp.sum(real * pr - imag * pi, axis=1)  85.3 us
    dot_general x1, matrix products, channelize(): jnp.einsum('kqbfn,kqnrj->krbfj', halfway, table, precision=lax.Precision....  65.5 us
    ppermute x1, waiting for transfers between devices, shifted_2(): return lax.ppermute(block, axis, route)  54.9 us
    unnamed x21, local copies, waits for them, and re-layouts  52.7 us
  transfers between devices with their start and end apart: 13, of which 12 were waited for; matrix products, arithmetic and copies ran while one was open for 23% of the time, Pallas kernels for 0%

profile of v1, /device:TPU:0, one launch (start us, length us, event | category | flops | bytes accessed | tf_op | source)
XLA Modules:
  0.0 1452.2 jit_solution(7291310825981093472)
XLA Ops:
  42.8 54.9 %collective-permute-done = bf16[2,64,12288]{2,1,0:T(8,128)(2,1)} collective-permute-done((bf16[2,64,12288]{2,1,0:T(8,128)(2,1)S(1)}, bf16[2,64,12288]{2,1,0:T(8,128)(2,1)}, u32[]{:S(2)}, u32[]{:S(2)}) %collective-permute-start) | collective-permute-done | bytes 3145760 | tf_op jit(solution)/shard_map/ppermute | solution.py:26
  97.7 35.9 %maximum_convert_fusion = f32[2,64,143360]{2,1,0:T(8,128)} fusion(bf16[2,64,131072]{2,1,0:T(8,128)(2,1)} %param.3, bf16[2,64,12288]{2,1,0:T(8,128)(2,1)} %collective-permute-done), kind=kLoop, calls=%fused_computation.55 | loop fusion | flops 73400320 | bytes 110100480 | tf_op jit(solution)/shard_map/convert_element_type | solution.py:63
  133.6 48.6 %copy.103 = f32[16,8,1120,128]{3,2,1,0:T(8,128)} copy(f32[16,8,1120,128]{3,1,2,0:T(8,128)} %bitcast.85) | data formatting | bytes 146800640
  182.3 47.7 %copy.112 = f32[2,64,35,32,128]{4,3,0,1,2:T(8,128)} copy(f32[2,64,35,32,128]{4,3,2,1,0:T(8,128)} %bitcast.87) | data formatting | bytes 146800640 | tf_op jit(solution)/shard_map/convert_element_type | solution.py:63
  230.0 112.3 %fusion.57 = f32[32,2,32,64,128,1]{4,0,3,2,1,5:T(8,128)} fusion(f32[2,32,35,64,128]{4,1,0,3,2:T(8,128)} %bitcast.278, f32[32,128]{1,0:T(8,128)S(1)} %get-tuple-element.57, f32[32,128]{1,0:T(8,128)S(1)} %get-tuple-element.58, f32[32,128]{1,0:T(8,128)S(1)} %get-tuple-element.59, f32[32,128]{1,0:T(8,128)S(1)} %get-tuple-element.56, ...), kind=kOutput, calls=%fused_computation.103 | convolution fusion | flops 6559895552 | bytes 335626240 | tf_op jit(solution)/shard_map/pmbfn,pmqk->kqbfn/dot_general | solution.py:68
  342.3 65.5 %fusion.10 = bf16[32,2,32,64,128]{4,3,2,1,0:T(8,128)(2,1)} fusion(f32[32,2,32,64,128,1]{4,0,3,2,1,5:T(8,128)} %fusion.57, f32[32,1,128,2,128]{4,2,1,3,0:T(8,128)} %get-tuple-element.45, f32[32,1,128,2,128]{4,2,1,3,0:T(8,128)} %get-tuple-element.44), kind=kOutput, calls=%fused_computation.56 | convolution fusion | flops 25788678144 | bytes 109051904 | tf_op jit(solution)/shard_map/kqbfn,kqnrj->krbfj/dot_general | solution.py:72
  415.5 21.5 %fusion.12 = (f32[32,32,128]{2,1,0:T(8,128)S(1)}, f32[32,32,128]{2,1,0:T(8,128)S(1)}) fusion(f32[32,64,128]{2,1,0:T(8,128)S(1)} %slice_bitcast_fusion.10, bf16[32,2,32,64,128]{4,3,2,1,0:T(8,128)(2,1)} %fusion.10), kind=kLoop, calls=%fused_computation.58 | loop fusion | flops 83623936 | bytes 35651584 | tf_op jit(solution)/shard_map/reduce_sum | solution.py:95
  438.6 84.0 %all-gather.14.cloned.1.call-done = f32[256,64,128]{2,1,0:T(8,128)} async-done(((f32[32,64,128]{2,1,0:T(8,128)}), f32[256,64,128]{2,1,0:T(8,128)}) %all-gather.14.cloned.1.call-update) | async-done | bytes 8388624 | tf_op jit(solution)/shard_map/all_gather | solution.py:17
  527.1 18.9 %fusion.16 = (f32[32,64,128]{2,1,0:T(8,128)S(1)}, f32[32,64,128]{2,1,0:T(8,128)S(1)}, f32[32,64,128]{2,1,0:T(8,128)S(1)}) fusion(f32[32,32,128]{2,1,0:T(8,128)S(1)} %get-tuple-element.55, f32[32,32,128]{2,1,0:T(8,128)S(1)} %get-tuple-element.54, bf16[32,2,32,64,128]{4,3,2,1,0:T(8,128)(2,1)} %fusion.10), kind=kLoop, calls=%fused_computation.62 | loop fusion | flops 116654080 | bytes 37748736 | tf_op jit(solution)/shard_map/reduce_sum | solution.py:106
  548.5 68.1 %all-reduce.5.cloned.1.call-done = f32[2,32,64,128]{3,2,1,0:T(8,128)} async-done(((f32[2,32,64,128]{3,2,1,0:T(8,128)}), f32[2,32,64,128]{3,2,1,0:T(8,128)}) %all-reduce.5.cloned.1.call-update) | async-done | bytes 2097168 | tf_op jit(solution)/shard_map/psum | solution.py:112
  618.3 21.4 %fusion.22 = (f32[32,32,128]{2,1,0:T(8,128)S(1)}, f32[32,32,128]{2,1,0:T(8,128)S(1)}) fusion(f32[32,64,128]{2,1,0:T(8,128)S(1)} %get-tuple-element.43, f32[32,64,128]{2,1,0:T(8,128)S(1)} %get-tuple-element.42, bf16[32,2,32,64,128]{4,3,2,1,0:T(8,128)(2,1)} %fusion.10), kind=kLoop, calls=%fused_computation.68 | loop fusion | flops 83623936 | bytes 36700160 | tf_op jit(solution)/shard_map/reduce_sum | solution.py:95
  641.5 83.0 %all-gather.16.cloned.1.call-done = f32[256,65,128]{2,0,1:T(8,128)} async-done(((f32[32,65,128]{2,0,1:T(8,128)}), f32[256,65,128]{2,0,1:T(8,128)}) %all-gather.16.cloned.1.call-update) | async-done | bytes 8519696 | tf_op jit(solution)/shard_map/all_gather | solution.py:17
  752.0 68.1 %all-reduce.7.cloned.1.call-done = f32[2,32,64,128]{3,2,1,0:T(8,128)} async-done(((f32[2,32,64,128]{3,2,1,0:T(8,128)}), f32[2,32,64,128]{3,2,1,0:T(8,128)}) %all-reduce.7.cloned.1.call-update) | async-done | bytes 2097168 | tf_op jit(solution)/shard_map/psum | solution.py:112
  821.9 21.4 %fusion.30 = (f32[32,32,128]{2,1,0:T(8,128)S(1)}, f32[32,32,128]{2,1,0:T(8,128)S(1)}) fusion(f32[32,64,128]{2,1,0:T(8,128)S(1)} %get-tuple-element.41, f32[32,64,128]{2,1,0:T(8,128)S(1)} %get-tuple-element.40, bf16[32,2,32,64,128]{4,3,2,1,0:T(8,128)(2,1)} %fusion.10), kind=kLoop, calls=%fused_computation.76 | loop fusion | flops 83623936 | bytes 36700160 | tf_op jit(solution)/shard_map/reduce_sum | solution.py:95
  845.0 83.0 %all-gather.18.cloned.1.call-done = f32[256,65,128]{2,0,1:T(8,128)} async-done(((f32[32,65,128]{2,0,1:T(8,128)}), f32[256,65,128]{2,0,1:T(8,128)}) %all-gather.18.cloned.1.call-update) | async-done | bytes 8519696 | tf_op jit(solution)/shard_map/all_gather | solution.py:17
  936.4 16.6 %fusion.34 = (f32[32,64,128]{2,1,0:T(8,128)S(1)}, f32[32,64,128]{2,1,0:T(8,128)S(1)}) fusion(f32[32,32,128]{2,1,0:T(8,128)S(1)} %copy.72, f32[32,32,128]{2,1,0:T(8,128)S(1)} %copy.71, bf16[32,2,32,64,128]{4,3,2,1,0:T(8,128)(2,1)} %fusion.10), kind=kLoop, calls=%fused_computation.80 | loop fusion | flops 83361792 | bytes 36700160 | tf_op jit(solution)/shard_map/reduce_sum | solution.py:106
  955.5 68.1 %all-reduce.9.cloned.1.call-done = f32[2,32,64,128]{3,2,1,0:T(8,128)} async-done(((f32[2,32,64,128]{3,2,1,0:T(8,128)}), f32[2,32,64,128]{3,2,1,0:T(8,128)}) %all-reduce.9.cloned.1.call-update) | async-done | bytes 2097168 | tf_op jit(solution)/shard_map/psum | solution.py:112
  1025.4 21.4 %fusion.38 = (f32[32,32,128]{2,1,0:T(8,128)S(1)}, f32[32,32,128]{2,1,0:T(8,128)S(1)}) fusion(f32[32,64,128]{2,1,0:T(8,128)S(1)} %get-tuple-element.39, f32[32,64,128]{2,1,0:T(8,128)S(1)} %get-tuple-element.38, bf16[32,2,32,64,128]{4,3,2,1,0:T(8,128)(2,1)} %fusion.10), kind=kLoop, calls=%fused_computation.84 | loop fusion | flops 83623936 | bytes 36700160 | tf_op jit(solution)/shard_map/reduce_sum | solution.py:95
  1048.6 83.0 %all-gather.20.cloned.1.call-done = f32[256,65,128]{2,0,1:T(8,128)} async-done(((f32[32,65,128]{2,0,1:T(8,128)}), f32[256,65,128]{2,0,1:T(8,128)}) %all-gather.20.cloned.1.call-update) | async-done | bytes 8519696 | tf_op jit(solution)/shard_map/all_gather | solution.py:17
  1159.1 68.1 %all-reduce.11.cloned.1.call-done = f32[2,32,64,128]{3,2,1,0:T(8,128)} async-done(((f32[2,32,64,128]{3,2,1,0:T(8,128)}), f32[2,32,64,128]{3,2,1,0:T(8,128)}) %all-reduce.11.cloned.1.call-update) | async-done | bytes 2097168 | tf_op jit(solution)/shard_map/psum | solution.py:112
  1228.9 21.4 %fusion.46 = (f32[32,32,128]{2,1,0:T(8,128)S(1)}, f32[32,32,128]{2,1,0:T(8,128)S(1)}) fusion(f32[32,64,128]{2,1,0:T(8,128)S(1)} %get-tuple-element.37, f32[32,64,128]{2,1,0:T(8,128)S(1)} %get-tuple-element.36, bf16[32,2,32,64,128]{4,3,2,1,0:T(8,128)(2,1)} %fusion.10), kind=kLoop, calls=%fused_computation.92 | loop fusion | flops 83623936 | bytes 36700160 | tf_op jit(solution)/shard_map/reduce_sum | solution.py:95
  1252.2 82.9 %all-gather.22.cloned.1.call-done = f32[256,65,128]{2,0,1:T(8,128)} async-done(((f32[32,65,128]{2,0,1:T(8,128)}), f32[256,65,128]{2,0,1:T(8,128)}) %all-gather.22.cloned.1.call-update) | async-done | bytes 8519696 | tf_op jit(solution)/shard_map/all_gather | solution.py:17
  1365.8 51.2 %reduce-scatter.2.cloned.1.call-done = f32[2,1024,64]{2,1,0:T(8,128)} async-done(((f32[2,4096,64]{2,1,0:T(8,128)}), f32[2,1024,64]{2,1,0:T(8,128)}) %reduce-scatter.2.cloned.1.call-update) | async-done | bytes 524304 | tf_op jit(solution)/shard_map/reduce_scatter | solution.py:114
  1420.2 19.7 %all_to_all.36 = f32[8,1,16384]{2,1,0:T(1,128)S(1)} all-to-all(f32[8,1,16384]{2,1,0:T(1,128)S(1)} %reshape.306), channel_id=1, replica_groups=mesh['section'=4,'chan'=8] {'chan'}, dimensions={0} | all-to-all | bytes 1048576 | tf_op jit(solution)/shard_map/all_to_all | solution.py:115
  (130 shorter events, 171.3 us)
Async XLA Ops:
  8.6 89.1 %collective-permute-start = (bf16[2,64,12288]{2,1,0:T(8,128)(2,1)S(1)}, bf16[2,64,12288]{2,1,0:T(8,128)(2,1)}, u32[]{:S(2)}, u32[]{:S(2)}) collective-permute-start(bf16[2,64,12288]{2,1,0:T(8,128)(2,1)S(1)} %slice.103), channel_id=1, source_target_pairs={{0,8},{8,16},{16,24},{1,9},{9,17},{17,25},{2,10},{10,18},{18,26},{... | collective-permute-start | bytes 9437192 | tf_op jit(solution)/shard_map/ppermute | solution.py:26
  20.3 20.3 %all-to-all-start = ((f32[2,128,512]{1,0,2:T(2,128)}), f32[2,128,512]{1,0,2:T(2,128)}, u32[]{:S(2)}, u32[]{:S(2)}) async-start(f32[2,128,512]{1,0,2:T(2,128)} %pad_maximum_fusion.9), calls=%async_computation | async-start | bytes 1048576 | tf_op jit(solution)/shard_map/all_to_all | solution.py:82
  25.2 382.6 %all-gather.12.cloned.1.call-start = ((), (), s32[]{:S(2)}) async-start(), calls=%async_computation.3 | async-start | bytes 2621440 | tf_op jit(solution)/shard_map/all_gather | solution.py:83
  42.6 480.1 %all-gather.14.cloned.1.call-start = ((), (), s32[]{:S(2)}) async-start(), calls=%async_computation.9 | async-start | bytes 9437184 | tf_op jit(solution)/shard_map/all_gather | solution.py:17
  438.1 178.4 %all-reduce.5.cloned.1.call-start = ((), (), s32[]{:S(2)}) async-start(), calls=%async_computation.4 | async-start | bytes 4194304 | tf_op jit(solution)/shard_map/psum | solution.py:112
  548.4 176.1 %all-gather.16.cloned.1.call-start = ((), (), s32[]{:S(2)}) async-start(), calls=%async_computation.10 | async-start | bytes 9584640 | tf_op jit(solution)/shard_map/all_gather | solution.py:17
  618.3 21.4 %copy-start.2 = (f32[2,32,64,128]{3,2,1,0:T(8,128)S(1)}, f32[2,32,64,128]{3,2,1,0:T(8,128)}, u32[]{:S(2)}) copy-start(f32[2,32,64,128]{3,2,1,0:T(8,128)} %all-reduce.5.cloned.1.call-done) | copy-start | bytes 6291460
  641.2 178.8 %all-reduce.7.cloned.1.call-start = ((), (), s32[]{:S(2)}) async-start(), calls=%async_computation.5 | async-start | bytes 4194304 | tf_op jit(solution)/shard_map/psum | solution.py:112
  732.9 16.6 %copy-start.3 = (f32[2,32,64,128]{3,2,1,0:T(8,128)S(1)}, f32[2,32,64,128]{3,2,1,0:T(8,128)}, u32[]{:S(2)}) copy-start(f32[2,32,64,128]{3,2,1,0:T(8,128)} %all-reduce.5.cloned.1.call-done) | copy-start | bytes 6291460
  751.9 176.1 %all-gather.18.cloned.1.call-start = ((), (), s32[]{:S(2)}) async-start(), calls=%async_computation.11 | async-start | bytes 9584640 | tf_op jit(solution)/shard_map/all_gather | solution.py:17
  821.9 21.4 %copy-start.4 = (f32[2,32,64,128]{3,2,1,0:T(8,128)S(1)}, f32[2,32,64,128]{3,2,1,0:T(8,128)}, u32[]{:S(2)}) copy-start(f32[2,32,64,128]{3,2,1,0:T(8,128)} %all-reduce.7.cloned.1.call-done) | copy-start | bytes 6291460
  844.8 178.8 %all-reduce.9.cloned.1.call-start = ((), (), s32[]{:S(2)}) async-start(), calls=%async_computation.6 | async-start | bytes 4194304 | tf_op jit(solution)/shard_map/psum | solution.py:112
  936.4 16.6 %copy-start.5 = (f32[2,32,64,128]{3,2,1,0:T(8,128)S(1)}, f32[2,32,64,128]{3,2,1,0:T(8,128)}, u32[]{:S(2)}) copy-start(f32[2,32,64,128]{3,2,1,0:T(8,128)} %all-reduce.7.cloned.1.call-done) | copy-start | bytes 6291460
  955.5 176.1 %all-gather.20.cloned.1.call-start = ((), (), s32[]{:S(2)}) async-start(), calls=%async_computation.12 | async-start | bytes 9584640 | tf_op jit(solution)/shard_map/all_gather | solution.py:17
  1025.4 21.4 %copy-start.6 = (f32[2,32,64,128]{3,2,1,0:T(8,128)S(1)}, f32[2,32,64,128]{3,2,1,0:T(8,128)}, u32[]{:S(2)}) copy-start(f32[2,32,64,128]{3,2,1,0:T(8,128)} %all-reduce.9.cloned.1.call-done) | copy-start | bytes 6291460
  1048.3 178.8 %all-reduce.11.cloned.1.call-start = ((), (), s32[]{:S(2)}) async-start(), calls=%async_computation.7 | async-start | bytes 4194304 | tf_op jit(solution)/shard_map/psum | solution.py:112
  1140.0 16.6 %copy-start.7 = (f32[2,32,64,128]{3,2,1,0:T(8,128)S(1)}, f32[2,32,64,128]{3,2,1,0:T(8,128)}, u32[]{:S(2)}) copy-start(f32[2,32,64,128]{3,2,1,0:T(8,128)} %all-reduce.9.cloned.1.call-done) | copy-start | bytes 6291460
  1159.0 176.1 %all-gather.22.cloned.1.call-start = ((), (), s32[]{:S(2)}) async-start(), calls=%async_computation.13 | async-start | bytes 9584640 | tf_op jit(solution)/shard_map/all_gather | solution.py:17
  1228.9 21.4 %copy-start = (f32[2,32,64,128]{3,2,1,0:T(8,128)S(1)}, f32[2,32,64,128]{3,2,1,0:T(8,128)}, u32[]{:S(2)}) copy-start(f32[2,32,64,128]{3,2,1,0:T(8,128)} %all-reduce.11.cloned.1.call-done) | copy-start | bytes 6291460
  1251.9 165.2 %reduce-scatter.2.cloned.1.call-start = ((), (), s32[]{:S(2)}) async-start(), calls=%async_computation.8 | async-start | bytes 5242880 | tf_op jit(solution)/shard_map/reduce_scatter | solution.py:114
  1343.5 16.6 %copy-start.1 = (f32[2,32,64,128]{3,2,1,0:T(8,128)S(1)}, f32[2,32,64,128]{3,2,1,0:T(8,128)}, u32[]{:S(2)}) copy-start(f32[2,32,64,128]{3,2,1,0:T(8,128)} %all-reduce.11.cloned.1.call-done) | copy-start | bytes 6291460
Sparse Core Ops, SparseCore 0:
  42.7 49.4 all-gather.11
  438.2 84.3 all-gather.13
  548.5 67.9 all-reduce.4
  641.4 83.0 all-gather.15
  752.1 67.9 all-reduce.6
  844.9 83.0 all-gather.17
  955.6 67.9 all-reduce.8
  1048.4 83.0 all-gather.19
  1159.2 67.9 all-reduce.10
  1252.0 83.0 all-gather.21
  1365.9 51.0 reduce-scatter.1
